TPU v7x, 32 devices: a whole 2x2x4 slice. The times are simulated.
32 devices in a mesh: seq: 8 (over y, x, core), head: 4 (over z).
Axes of the slice: x: 2, y: 2, z: 4, core: 2. Of those that a mesh axis runs over, the one named last changes fastest.
Arguments:
- tokens: bfloat16 [32, 1024, 1024], P('seq'), may hold values from -6 to 6
- w_query: bfloat16 [1024, 1024], P(None, 'head'), may hold values from -1 to 1
- w_key: bfloat16 [1024, 1024], P(None, 'head'), may hold values from -1 to 1
- w_value: bfloat16 [1024, 1024], P(None, 'head'), may hold values from -0.1875 to 0.1875
- w_out: bfloat16 [1024, 1024], P('head'), may hold values from -0.1875 to 0.1875
Outputs:
- mixed: bfloat16 [32, 1024, 1024], P('seq', None, 'head')
All inputs are finite; a program needn't handle non-finite values.
Results may differ from a plain program's by a relative error of at most 0.012.
Values may be sent and summed in bfloat16 or wider, within the bound.
No kernel may reach another device: no remote copies, remote signals or barrier semaphores. Data moves between devices by JAX's collectives and lax.ppermute only.
A program may use at most 128 MiB of HBM per device.

v0:
```python
import jax
import jax.numpy as jnp
from jax import lax
from jax.sharding import PartitionSpec as P

HS = 64
epsilon = 1e-05


def normalize(tokens):
    values = tokens.astype(jnp.float32)
    row_mean = jnp.mean(values, axis=-1, keepdims=True)
    centered = values - row_mean
    row_var = jnp.mean(centered * centered, axis=-1, keepdims=True)
    return (centered * lax.rsqrt(row_var + epsilon)).astype(jnp.bfloat16)


def project(source, weight):
    return jnp.einsum("fpd,dc->fpc", source, weight, preferred_element_type=jnp.float32).astype(
        jnp.bfloat16
    )


def attend(queries, key_rows, value_rows, head_count):
    frames, patch_count, feature_width = queries.shape
    head_size = feature_width // head_count
    query_flat = queries.reshape(frames, patch_count * head_count, head_size)
    key_flat = key_rows.reshape(frames, patch_count * head_count, head_size)
    value_flat = value_rows.reshape(frames, patch_count * head_count, head_size)
    scores = jnp.einsum(
        "fmd,gmd->fgm", query_flat, key_flat, preferred_element_type=jnp.float32
    ) * head_size ** (-0.5)
    row_top = jnp.max(scores, axis=1, keepdims=True)
    raised = jnp.exp(scores - row_top)
    weights = (raised / jnp.sum(raised, axis=1, keepdims=True)).astype(jnp.bfloat16)
    attended = jnp.einsum("fgm,gmd->fmd", weights, value_flat, preferred_element_type=jnp.float32)
    return attended.astype(jnp.bfloat16).reshape(frames, patch_count, feature_width)


def local(tokens, w_query, w_key, w_value, w_out):
    normed = normalize(tokens)
    head_count = w_query.shape[1] // HS
    local_query = project(normed, w_query)
    local_key = project(normed, w_key)
    local_value = project(normed, w_value)
    queries, key_rows, value_rows = (
        lax.all_to_all(local_query, "seq", split_axis=1, concat_axis=0, tiled=True),
        lax.all_to_all(local_key, "seq", split_axis=1, concat_axis=0, tiled=True),
        lax.all_to_all(local_value, "seq", split_axis=1, concat_axis=0, tiled=True),
    )
    attended = attend(queries, key_rows, value_rows, head_count)
    partial_value = jnp.einsum("fpc,cd->fpd", attended, w_out, preferred_element_type=jnp.float32)
    columns = lax.psum_scatter(
        partial_value.astype(jnp.bfloat16), "head", scatter_dimension=2, tiled=True
    )
    return lax.all_to_all(columns, "seq", split_axis=0, concat_axis=1, tiled=True)


def solution(mesh):
    return jax.shard_map(
        local,
        mesh=mesh,
        in_specs=(
            P("seq", None, None),
            P(None, "head"),
            P(None, "head"),
            P(None, "head"),
            P("head", None),
        ),
        out_specs=P("seq", None, "head"),
        check_vma=False,
    )
```

profile of v0, /device:TPU:0, one launch (start us, length us, event | category | flops | bytes accessed | tf_op | source)
XLA Modules:
  0.0 326.3 jit_solution(13314724638309537397)
XLA Ops:
  6.5 0.0 copy-start
  6.5 0.0 copy-start.1
  6.5 0.0 copy-start.3
  6.5 4.7 %convert_reduce_fusion = f32[4,1024]{1,0:T(4,128)S(1)} fusion(bf16[4,1024,1024]{2,1,0:T(8,128)(2,1)} %param.5), kind=kLoop, calls=%fused_computation.2 | loop fusion | flops 8384512 | bytes 8404992 | tf_op jit(solution)/shard_map/reduce_sum | solution.py:12
  11.3 1.1 copy-done.1
  12.4 2.8 fusion.3
  15.2 0.0 copy-done.3
  15.2 3.1 fusion.28
  18.3 0.0 copy-start.4
  18.4 3.0 copy.19
  21.3 5.2 %all-to-all-start.1 = ((bf16[4,1024,256]{2,0,1:T(4,128)(2,1)}), bf16[4,1024,256]{2,0,1:T(4,128)(2,1)S(1)}, u32[]{:S(2)}, u32[]{:S(2)}) async-start(bf16[4,1024,256]{2,0,1:T(4,128)(2,1)} %copy.19), calls=%async_computation.1 | async-start | bytes 4194304 | tf_op jit(solution)/shard_map/all_to_all | solution.py:48
  26.5 0.0 copy-done.4
  26.5 5.0 %fusion.31 = bf16[4,1024,256]{2,1,0:T(8,128)(2,1)S(1)} fusion(bf16[4,1024,1024]{2,1,0:T(8,128)(2,1)} %param.5, f32[4,1024]{1,0:T(4,128)S(1)} %add_rsqrt_fusion, f32[4,1024]{1,0:T(4,128)S(1)} %broadcast_multiply_fusion, bf16[1024,256]{1,0:T(8,128)(2,1)S(1)} %copy-done.4), kind=kOutput, calls=%fused_computation.30 | convolution fusion | flops 2165309440 | bytes 11042816 | tf_op jit(solution)/shard_map/fpd,dc->fpc/dot_general | solution.py:19
  31.5 0.0 copy-start.5
  31.6 2.9 copy.21
  34.5 18.6 %all-to-all-done.1 = bf16[4,1024,256]{2,0,1:T(4,128)(2,1)S(1)} async-done(((bf16[4,1024,256]{2,0,1:T(4,128)(2,1)}), bf16[4,1024,256]{2,0,1:T(4,128)(2,1)S(1)}, u32[]{:S(2)}, u32[]{:S(2)}) %all-to-all-start.1) | async-done | bytes 2097184 | tf_op jit(solution)/shard_map/all_to_all | solution.py:48
  53.1 0.0 copy-start.2
  53.1 4.3 %all-to-all-start.2 = ((bf16[4,1024,256]{2,0,1:T(4,128)(2,1)}), bf16[4,1024,256]{2,0,1:T(4,128)(2,1)}, u32[]{:S(2)}, u32[]{:S(2)}) async-start(bf16[4,1024,256]{2,0,1:T(4,128)(2,1)} %copy.21), calls=%async_computation.2 | async-start | bytes 4194304 | tf_op jit(solution)/shard_map/all_to_all | solution.py:47
  57.5 0.0 copy-done.5
  57.5 5.0 %fusion.25 = bf16[4,1024,256]{2,1,0:T(8,128)(2,1)S(1)} fusion(bf16[4,1024,1024]{2,1,0:T(8,128)(2,1)} %param.5, f32[4,1024]{1,0:T(4,128)S(1)} %add_rsqrt_fusion, f32[4,1024]{1,0:T(4,128)S(1)} %broadcast_multiply_fusion, bf16[1024,256]{1,0:T(8,128)(2,1)S(1)} %copy-done.5), kind=kOutput, calls=%fused_computation.28 | convolution fusion | flops 2165309440 | bytes 11042816 | tf_op jit(solution)/shard_map/fpd,dc->fpc/dot_general | solution.py:19
  62.5 0.0 copy-done.2
  62.5 2.9 copy.17
  65.5 18.7 %all-to-all-done.2 = bf16[4,1024,256]{2,0,1:T(4,128)(2,1)} async-done(((bf16[4,1024,256]{2,0,1:T(4,128)(2,1)}), bf16[4,1024,256]{2,0,1:T(4,128)(2,1)}, u32[]{:S(2)}, u32[]{:S(2)}) %all-to-all-start.2) | async-done | bytes 2097184 | tf_op jit(solution)/shard_map/all_to_all | solution.py:47
  84.1 4.4 %all-to-all-start = ((bf16[4,1024,256]{2,0,1:T(4,128)(2,1)}), bf16[4,1024,256]{2,0,1:T(4,128)(2,1)}, u32[]{:S(2)}, u32[]{:S(2)}) async-start(bf16[4,1024,256]{2,0,1:T(4,128)(2,1)} %copy.17), calls=%async_computation | async-start | bytes 4194304 | tf_op jit(solution)/shard_map/all_to_all | solution.py:49
  88.5 0.2 reduce-scatter.2.cloned.1.call-start
  88.7 2.0 copy.42
  90.7 3.3 reshape.30
  94.0 2.0 copy.41
  95.9 3.2 reshape.31
  99.2 8.3 %fusion.18 = f32[512,32,32]{2,1,0:T(8,128)S(1)} fusion(bf16[32,512,64]{2,1,0:T(8,128)(2,1)} %reshape.31, bf16[32,512,64]{2,1,0:T(8,128)(2,1)} %reshape.30), kind=kOutput, calls=%fused_computation.19 | convolution fusion | flops 67108864 | bytes 6291456 | tf_op jit(solution)/shard_map/fmd,gmd->fgm/dot_general | solution.py:30
  107.5 6.1 %fusion.39 = (f32[32,512]{0,1:T(8,128)S(1)}, f32[32,32,512]{0,1,2:T(8,128)}) fusion(f32[512,32,32]{2,1,0:T(8,128)S(1)} %fusion.18), kind=kOutput, calls=%fused_computation.38 | output fusion | flops 2097183 | bytes 4259840 | tf_op jit(solution)/shard_map/sub | solution.py:34
  113.6 1.5 all-to-all-done
  115.1 2.0 copy.43
  117.1 3.3 %reshape.29 = bf16[32,512,64]{2,1,0:T(8,128)(2,1)} reshape(bf16[8,4,128,256]{3,2,1,0:T(8,128)(2,1)S(1)} %bitcast.50) | data formatting | bytes 4194304 | tf_op jit(solution)/shard_map/reshape | solution.py:29
  120.4 8.1 %convert_bitcast_fusion = bf16[32,512,64]{2,0,1:T(8,128)(2,1)S(1)} fusion(f32[32,32,512]{0,1,2:T(8,128)} %get-tuple-element.6, f32[32,512]{0,1:T(8,128)S(1)} %get-tuple-element.5, bf16[32,512,64]{2,1,0:T(8,128)(2,1)} %reshape.29), kind=kOutput, calls=%fused_computation.22 | convolution fusion | flops 69206016 | bytes 6356992 | tf_op jit(solution)/shard_map/fgm,gmd->fmd/dot_general | solution.py:36
  128.5 3.6 %copy.27 = bf16[32,512,64]{2,1,0:T(8,128)(2,1)} copy(bf16[32,512,64]{2,0,1:T(8,128)(2,1)S(1)} %convert_bitcast_fusion) | data formatting | bytes 4194304 | tf_op jit(solution)/shard_map/convert_element_type | solution.py:37
  132.1 5.5 %reshape.32 = bf16[32,128,256]{2,1,0:T(8,128)(2,1)S(1)} reshape(bf16[32,512,64]{2,1,0:T(8,128)(2,1)} %copy.27) | data formatting | bytes 4194304 | tf_op jit(solution)/shard_map/reshape | solution.py:37
  137.6 0.0 copy-done
  137.6 5.6 %convolution_convert_fusion = bf16[32,128,1024]{2,1,0:T(8,128)(2,1)} fusion(bf16[32,128,256]{2,1,0:T(8,128)(2,1)S(1)} %reshape.32, bf16[256,1024]{1,0:T(8,128)(2,1)S(1)} %copy-done), kind=kOutput, calls=%fused_computation.13 | convolution fusion | flops 2151677952 | bytes 11010048 | tf_op jit(solution)/shard_map/fpc,cd->fpd/dot_general | solution.py:52
  143.1 0.0 reduce-scatter.2.cloned.1.call-update
  143.2 144.7 %reduce-scatter.2.cloned.1.call-done = bf16[32,128,256]{2,1,0:T(8,128)(2,1)} async-done(((bf16[32,128,1024]{2,1,0:T(8,128)(2,1)}), bf16[32,128,256]{2,1,0:T(8,128)(2,1)}) %reduce-scatter.2.cloned.1.call-update) | async-done | bytes 2097168 | tf_op jit(solution)/shard_map/reduce_scatter | solution.py:53
  287.8 30.2 %all_to_all.63 = bf16[32,128,256]{2,1,0:T(8,128)(2,1)S(1)} all-to-all(bf16[32,128,256]{2,1,0:T(8,128)(2,1)} %reduce-scatter.2.cloned.1.call-done), channel_id=1, replica_groups=mesh['seq'=8,'head'=4] {'seq'}, dimensions={0} | all-to-all | bytes 4194304 | tf_op jit(solution)/shard_map/all_to_all | solution.py:56
  318.0 1.5 copy.28
  (2 shorter events, 0.0 us)
Async XLA Ops:
  6.5 131.0 %copy-start = (bf16[256,1024]{1,0:T(8,128)(2,1)S(1)}, bf16[256,1024]{1,0:T(8,128)(2,1)}, u32[]{:S(2)}) copy-start(bf16[256,1024]{1,0:T(8,128)(2,1)} %param.9) | copy-start | bytes 1572868
  6.5 5.8 %copy-start.1 = (bf16[4,1024,1024]{2,1,0:T(8,128)(2,1)S(1)}, bf16[4,1024,1024]{2,1,0:T(8,128)(2,1)}, u32[]{:S(2)}) copy-start(bf16[4,1024,1024]{2,1,0:T(8,128)(2,1)} %param.5) | copy-start | bytes 25165828
  6.5 8.6 %copy-start.3 = (bf16[1024,256]{1,0:T(8,128)(2,1)S(1)}, bf16[1024,256]{1,0:T(8,128)(2,1)}, u32[]{:S(2)}) copy-start(bf16[1024,256]{1,0:T(8,128)(2,1)} %param.7) | copy-start | bytes 1572868
  18.3 8.2 %copy-start.4 = (bf16[1024,256]{1,0:T(8,128)(2,1)S(1)}, bf16[1024,256]{1,0:T(8,128)(2,1)}, u32[]{:S(2)}) copy-start(bf16[1024,256]{1,0:T(8,128)(2,1)} %param.6) | copy-start | bytes 1572868
  21.3 31.8 %all-to-all-start.1 = ((bf16[4,1024,256]{2,0,1:T(4,128)(2,1)}), bf16[4,1024,256]{2,0,1:T(4,128)(2,1)S(1)}, u32[]{:S(2)}, u32[]{:S(2)}) async-start(bf16[4,1024,256]{2,0,1:T(4,128)(2,1)} %copy.19), calls=%async_computation.1 | async-start | bytes 4194304 | tf_op jit(solution)/shard_map/all_to_all | solution.py:48
  31.5 25.9 %copy-start.5 = (bf16[1024,256]{1,0:T(8,128)(2,1)S(1)}, bf16[1024,256]{1,0:T(8,128)(2,1)}, u32[]{:S(2)}) copy-start(bf16[1024,256]{1,0:T(8,128)(2,1)} %param.8) | copy-start | bytes 1572868
  53.1 9.4 %copy-start.2 = (bf16[4,1024,256]{2,0,1:T(4,128)(2,1)}, bf16[4,1024,256]{2,0,1:T(4,128)(2,1)S(1)}, u32[]{:S(2)}) copy-start(bf16[4,1024,256]{2,0,1:T(4,128)(2,1)S(1)} %all-to-all-done.1) | copy-start | bytes 6291460
  53.1 31.0 %all-to-all-start.2 = ((bf16[4,1024,256]{2,0,1:T(4,128)(2,1)}), bf16[4,1024,256]{2,0,1:T(4,128)(2,1)}, u32[]{:S(2)}, u32[]{:S(2)}) async-start(bf16[4,1024,256]{2,0,1:T(4,128)(2,1)} %copy.21), calls=%async_computation.2 | async-start | bytes 4194304 | tf_op jit(solution)/shard_map/all_to_all | solution.py:47
  84.1 31.0 %all-to-all-start = ((bf16[4,1024,256]{2,0,1:T(4,128)(2,1)}), bf16[4,1024,256]{2,0,1:T(4,128)(2,1)}, u32[]{:S(2)}, u32[]{:S(2)}) async-start(bf16[4,1024,256]{2,0,1:T(4,128)(2,1)} %copy.17), calls=%async_computation | async-start | bytes 4194304 | tf_op jit(solution)/shard_map/all_to_all | solution.py:49
  88.5 199.3 %reduce-scatter.2.cloned.1.call-start = ((), (), s32[]{:S(2)}) async-start(), calls=%async_computation.5 | async-start | bytes 10485760 | tf_op jit(solution)/shard_map/reduce_scatter | solution.py:53
Sparse Core Ops, SparseCore 0:
  143.3 144.4 reduce-scatter.1
where the time goes:
time: 327 us; the launch traced here: 326 us
  waiting for transfers between devices  184 us (56%)
  local copies, waits for them, and re-layouts  36.1 us (11%)
  matrix products  35.2 us (11%)
  blocking collectives  30.2 us (9%)
  starting transfers between devices  14.1 us (4%)
  other arithmetic  13.6 us (4%)
  between operations  13.6 us (4%)
    reduce_scatter x1, waiting for transfers between devices, local(): lax.psum_scatter(partial_value.astype(jnp.bfloat16), 'head', scatter_dime...  145 us
    all_to_all x1, blocking collectives, local(): lax.all_to_all(columns, 'seq', split_axis=0, concat_axis=1, tiled=True)  30.2 us
    all_to_all x1, waiting for transfers between devices, local(): lax.all_to_all(local_query, 'seq', split_axis=1, concat_axis=0, tiled=True)  18.7 us
    all_to_all x1, waiting for transfers between devices, local(): lax.all_to_all(local_key, 'seq', split_axis=1, concat_axis=0, tiled=True)  18.6 us
    dot_general x3, matrix products, project(): jnp.einsum('fpd,dc->fpc', source, weight, preferred_element_type=jnp.floa...  13.2 us
    convert_element_type x3, local copies, waits for them, and re-layouts, project(): jnp.einsum('fpd,dc->fpc', source, weight, preferred_element_type=jnp.floa...  8.83 us
    dot_general x1, matrix products, attend(): jnp.einsum('fmd,gmd->fgm', query_flat, key_flat, preferred_element_type=j...  8.29 us
    dot_general x1, matrix products, attend(): jnp.einsum('fgm,gmd->fmd', weights, value_flat, preferred_element_type=jn...  8.14 us
  transfers between devices with their start and end apart: 4, of which 4 were waited for; matrix products, arithmetic and copies ran while one was open for 12% of the time, Pallas kernels for 0%

commit v1 on v0

--- a/solution.py
+++ b/solution.py
@@ -44,7 +44,12 @@
     local_key = project(normed, w_key)
     local_value = project(normed, w_value)
     queries, key_rows, value_rows = (
-        lax.all_to_all(local_query, "seq", split_axis=1, concat_axis=0, tiled=True),
+        jnp.concatenate(
+            lax.all_to_all(
+                jnp.stack(jnp.split(local_query, lax.axis_size("seq"), axis=1)), "seq", 0, 0
+            ),
+            axis=0,
+        ),
         lax.all_to_all(local_key, "seq", split_axis=1, concat_axis=0, tiled=True),
         lax.all_to_all(local_value, "seq", split_axis=1, concat_axis=0, tiled=True),
     )

time: 327 us -> 332 us (1.015)
  local copies, waits for them, and re-layouts: 36.1 us -> 41.2 us
    unnamed x12 -> x17, local copies, waits for them, and re-layouts: 1.13 us -> 6.16 us
    another operation x0 -> x2, local copies, waits for them, and re-layouts: none -> 3.96 us  [the longest x1 3.24 us: attend(): query_flat = queries.reshape(frames, patch_count * head_count, head_size)]
    convert_element_type x3 -> x2, local copies, waits for them, and re-layouts: 8.83 us -> 5.94 us  [project(): jnp.einsum('fpd,dc->fpc', source, weight, preferred_element_type=jnp.floa...]
  transfers between devices with their start and end apart: 4 -> 4, of which waited for: 4 -> 3; matrix products, arithmetic and copies ran while one was open for 12% -> 13% of each run, Pallas kernels for 0% -> 0%
where the time goes in v1:
time: 332 us; the launch traced here: 331 us
  waiting for transfers between devices  183 us (55%)
  local copies, waits for them, and re-layouts  41.2 us (12%)
  matrix products  35.2 us (11%)
  blocking collectives  30.2 us (9%)
  starting transfers between devices  14.1 us (4%)
  other arithmetic  13.6 us (4%)
  between operations  13.5 us (4%)
    reduce_scatter x1, waiting for transfers between devices, local(): lax.psum_scatter(partial_value.astype(jnp.bfloat16), 'head', scatter_dime...  146 us
    all_to_all x1, blocking collectives, local(): lax.all_to_all(columns, 'seq', split_axis=0, concat_axis=1, tiled=True)  30.2 us
    all_to_all x1, waiting for transfers between devices, local(): lax.all_to_all(jnp.stack(jnp.split(local_query, lax.axis_size('seq'), axi...  18.6 us
    all_to_all x1, waiting for transfers between devices, local(): lax.all_to_all(local_key, 'seq', split_axis=1, concat_axis=0, tiled=True)  18.6 us
    dot_general x3, matrix products, project(): jnp.einsum('fpd,dc->fpc', source, weight, preferred_element_type=jnp.floa...  13.2 us
    dot_general x1, matrix products, attend(): jnp.einsum('fmd,gmd->fgm', query_flat, key_flat, preferred_element_type=j...  8.29 us
    dot_general x1, matrix products, attend(): jnp.einsum('fgm,gmd->fmd', weights, value_flat, preferred_element_type=jn...  8.14 us
  transfers between devices with their start and end apart: 4, of which 3 were waited for; matrix products, arithmetic and copies ran while one was open for 13% of the time, Pallas kernels for 0%

profile of v1, /device:TPU:0, one launch (start us, length us, event | category | flops | bytes accessed | tf_op | source)
XLA Modules:
  0.0 331.3 jit_solution(5498397499132221036)
XLA Ops:
  6.5 0.0 copy-start
  6.5 0.0 copy-start.1
  6.5 4.7 %convert_reduce_fusion = f32[4,1024]{1,0:T(4,128)S(1)} fusion(bf16[4,1024,1024]{2,1,0:T(8,128)(2,1)} %param.5), kind=kLoop, calls=%fused_computation.2 | loop fusion | flops 8384512 | bytes 8404992 | tf_op jit(solution)/shard_map/reduce_sum | solution.py:12
  11.3 1.1 copy-done.1
  12.4 0.0 copy-start.2
  12.4 2.8 fusion.3
  15.2 0.0 copy-done.2
  15.2 3.2 fusion.31
  18.4 0.0 copy-start.3
  18.4 0.7 fusion.45
  19.1 0.7 fusion.44
  19.8 0.7 fusion.43
  20.5 0.7 fusion.42
  21.2 0.7 fusion.41
  22.0 0.7 fusion.40
  22.7 0.7 fusion.39
  23.4 0.7 fusion.38
  24.1 5.2 %all-to-all-start.2 = ((bf16[8,4,128,256]{3,2,1,0:T(8,128)(2,1)}), bf16[8,4,128,256]{3,2,1,0:T(8,128)(2,1)S(1)}, u32[]{:S(2)}, u32[]{:S(2)}) async-start(bf16[8,4,128,256]{3,2,1,0:T(8,128)(2,1)} %fusion.38), calls=%async_computation.2 | async-start | bytes 4194304 | tf_op jit(solution)/shard_map/all_to_all | solution.py:48
  29.3 0.0 copy-done.3
  29.3 5.0 %fusion.28 = bf16[4,1024,256]{2,1,0:T(8,128)(2,1)S(1)} fusion(bf16[4,1024,1024]{2,1,0:T(8,128)(2,1)} %param.5, f32[4,1024]{1,0:T(4,128)S(1)} %add_rsqrt_fusion, f32[4,1024]{1,0:T(4,128)S(1)} %broadcast_multiply_fusion, bf16[1024,256]{1,0:T(8,128)(2,1)S(1)} %copy-done.3), kind=kOutput, calls=%fused_computation.28 | convolution fusion | flops 2165309440 | bytes 11042816 | tf_op jit(solution)/shard_map/fpd,dc->fpc/dot_general | solution.py:19
  34.3 0.0 copy-start.4
  34.4 2.9 copy.19
  37.3 18.6 %all-to-all-done.2 = bf16[8,4,128,256]{3,2,1,0:T(8,128)(2,1)S(1)} async-done(((bf16[8,4,128,256]{3,2,1,0:T(8,128)(2,1)}), bf16[8,4,128,256]{3,2,1,0:T(8,128)(2,1)S(1)}, u32[]{:S(2)}, u32[]{:S(2)}) %all-to-all-start.2) | async-done | bytes 2097184 | tf_op jit(solution)/shard_map/all_to_all | solution.py:48
  55.9 4.3 %all-to-all-start.1 = ((bf16[4,1024,256]{2,0,1:T(4,128)(2,1)}), bf16[4,1024,256]{2,0,1:T(4,128)(2,1)}, u32[]{:S(2)}, u32[]{:S(2)}) async-start(bf16[4,1024,256]{2,0,1:T(4,128)(2,1)} %copy.19), calls=%async_computation.1 | async-start | bytes 4194304 | tf_op jit(solution)/shard_map/all_to_all | solution.py:53
  60.3 0.0 copy-done.4
  60.3 5.0 %fusion.25 = bf16[4,1024,256]{2,1,0:T(8,128)(2,1)S(1)} fusion(bf16[4,1024,1024]{2,1,0:T(8,128)(2,1)} %param.5, f32[4,1024]{1,0:T(4,128)S(1)} %add_rsqrt_fusion, f32[4,1024]{1,0:T(4,128)S(1)} %broadcast_multiply_fusion, bf16[1024,256]{1,0:T(8,128)(2,1)S(1)} %copy-done.4), kind=kOutput, calls=%fused_computation.27 | convolution fusion | flops 2165309440 | bytes 11042816 | tf_op jit(solution)/shard_map/fpd,dc->fpc/dot_general | solution.py:19
  65.3 3.0 copy.17
  68.3 18.6 %all-to-all-done.1 = bf16[4,1024,256]{2,0,1:T(4,128)(2,1)} async-done(((bf16[4,1024,256]{2,0,1:T(4,128)(2,1)}), bf16[4,1024,256]{2,0,1:T(4,128)(2,1)}, u32[]{:S(2)}, u32[]{:S(2)}) %all-to-all-start.1) | async-done | bytes 2097184 | tf_op jit(solution)/shard_map/all_to_all | solution.py:53
  86.9 4.4 %all-to-all-start = ((bf16[4,1024,256]{2,0,1:T(4,128)(2,1)}), bf16[4,1024,256]{2,0,1:T(4,128)(2,1)}, u32[]{:S(2)}, u32[]{:S(2)}) async-start(bf16[4,1024,256]{2,0,1:T(4,128)(2,1)} %copy.17), calls=%async_computation | async-start | bytes 4194304 | tf_op jit(solution)/shard_map/all_to_all | solution.py:54
  91.3 0.2 reduce-scatter.2.cloned.1.call-start
  91.5 3.3 copy.38
  94.8 6.1 %reshape.26 = bf16[32,512,64]{2,1,0:T(8,128)(2,1)} reshape(bf16[8,4,128,256]{3,2,1,0:T(8,128)(2,1)} %bitcast.76) | data formatting | bytes 4194304 | tf_op jit(solution)/shard_map/reshape | solution.py:28
  100.9 3.2 reshape_reshape.3
  104.2 8.3 %fusion.18 = f32[512,32,32]{2,1,0:T(8,128)S(1)} fusion(bf16[32,512,64]{2,1,0:T(8,128)(2,1)} %reshape_reshape.3, bf16[32,512,64]{2,1,0:T(8,128)(2,1)} %reshape.26), kind=kOutput, calls=%fused_computation.19 | convolution fusion | flops 67108864 | bytes 6291456 | tf_op jit(solution)/shard_map/fmd,gmd->fgm/dot_general | solution.py:30
  112.5 6.1 %fusion.47 = (f32[32,512]{0,1:T(8,128)S(1)}, f32[32,32,512]{0,1,2:T(8,128)}) fusion(f32[512,32,32]{2,1,0:T(8,128)S(1)} %fusion.18), kind=kOutput, calls=%fused_computation.53 | output fusion | flops 2097183 | bytes 4259840 | tf_op jit(solution)/shard_map/sub | solution.py:34
  118.6 0.0 all-to-all-done
  118.6 2.0 copy.39
  120.6 3.3 reshape.25
  123.9 8.1 %convert_bitcast_fusion = bf16[32,512,64]{2,0,1:T(8,128)(2,1)S(1)} fusion(f32[32,32,512]{0,1,2:T(8,128)} %get-tuple-element.6, f32[32,512]{0,1:T(8,128)S(1)} %get-tuple-element.5, bf16[32,512,64]{2,1,0:T(8,128)(2,1)} %reshape.25), kind=kOutput, calls=%fused_computation.22 | convolution fusion | flops 69206016 | bytes 6356992 | tf_op jit(solution)/shard_map/fgm,gmd->fmd/dot_general | solution.py:36
  132.0 3.6 %copy.25 = bf16[32,512,64]{2,1,0:T(8,128)(2,1)} copy(bf16[32,512,64]{2,0,1:T(8,128)(2,1)S(1)} %convert_bitcast_fusion) | data formatting | bytes 4194304 | tf_op jit(solution)/shard_map/convert_element_type | solution.py:37
  135.6 5.5 %reshape.27 = bf16[32,128,256]{2,1,0:T(8,128)(2,1)S(1)} reshape(bf16[32,512,64]{2,1,0:T(8,128)(2,1)} %copy.25) | data formatting | bytes 4194304 | tf_op jit(solution)/shard_map/reshape | solution.py:37
  141.1 0.0 copy-done
  141.1 5.6 %convolution_convert_fusion = bf16[32,128,1024]{2,1,0:T(8,128)(2,1)} fusion(bf16[32,128,256]{2,1,0:T(8,128)(2,1)S(1)} %reshape.27, bf16[256,1024]{1,0:T(8,128)(2,1)S(1)} %copy-done), kind=kOutput, calls=%fused_computation.13 | convolution fusion | flops 2151677952 | bytes 11010048 | tf_op jit(solution)/shard_map/fpc,cd->fpd/dot_general | solution.py:57
  146.6 0.0 reduce-scatter.2.cloned.1.call-update
  146.7 146.2 %reduce-scatter.2.cloned.1.call-done = bf16[32,128,256]{2,1,0:T(8,128)(2,1)} async-done(((bf16[32,128,1024]{2,1,0:T(8,128)(2,1)}), bf16[32,128,256]{2,1,0:T(8,128)(2,1)}) %reduce-scatter.2.cloned.1.call-update) | async-done | bytes 2097168 | tf_op jit(solution)/shard_map/reduce_scatter | solution.py:58
  292.8 30.2 %all_to_all.53 = bf16[32,128,256]{2,1,0:T(8,128)(2,1)S(1)} all-to-all(bf16[32,128,256]{2,1,0:T(8,128)(2,1)} %reduce-scatter.2.cloned.1.call-done), channel_id=1, replica_groups=mesh['seq'=8,'head'=4] {'seq'}, dimensions={0} | all-to-all | bytes 4194304 | tf_op jit(solution)/shard_map/all_to_all | solution.py:61
  323.0 1.5 copy.26
  (2 shorter events, 0.0 us)
Async XLA Ops:
  6.5 134.5 %copy-start = (bf16[256,1024]{1,0:T(8,128)(2,1)S(1)}, bf16[256,1024]{1,0:T(8,128)(2,1)}, u32[]{:S(2)}) copy-start(bf16[256,1024]{1,0:T(8,128)(2,1)} %param.9) | copy-start | bytes 1572868
  6.5 5.8 %copy-start.1 = (bf16[4,1024,1024]{2,1,0:T(8,128)(2,1)S(1)}, bf16[4,1024,1024]{2,1,0:T(8,128)(2,1)}, u32[]{:S(2)}) copy-start(bf16[4,1024,1024]{2,1,0:T(8,128)(2,1)} %param.5) | copy-start | bytes 25165828
  12.4 2.8 copy-start.2
  18.4 11.0 %copy-start.3 = (bf16[1024,256]{1,0:T(8,128)(2,1)S(1)}, bf16[1024,256]{1,0:T(8,128)(2,1)}, u32[]{:S(2)}) copy-start(bf16[1024,256]{1,0:T(8,128)(2,1)} %param.7) | copy-start | bytes 1572868
  24.1 31.8 %all-to-all-start.2 = ((bf16[8,4,128,256]{3,2,1,0:T(8,128)(2,1)}), bf16[8,4,128,256]{3,2,1,0:T(8,128)(2,1)S(1)}, u32[]{:S(2)}, u32[]{:S(2)}) async-start(bf16[8,4,128,256]{3,2,1,0:T(8,128)(2,1)} %fusion.38), calls=%async_computation.2 | async-start | bytes 4194304 | tf_op jit(solution)/shard_map/all_to_all | solution.py:48
  34.3 25.9 %copy-start.4 = (bf16[1024,256]{1,0:T(8,128)(2,1)S(1)}, bf16[1024,256]{1,0:T(8,128)(2,1)}, u32[]{:S(2)}) copy-start(bf16[1024,256]{1,0:T(8,128)(2,1)} %param.8) | copy-start | bytes 1572868
  55.9 31.0 %all-to-all-start.1 = ((bf16[4,1024,256]{2,0,1:T(4,128)(2,1)}), bf16[4,1024,256]{2,0,1:T(4,128)(2,1)}, u32[]{:S(2)}, u32[]{:S(2)}) async-start(bf16[4,1024,256]{2,0,1:T(4,128)(2,1)} %copy.19), calls=%async_computation.1 | async-start | bytes 4194304 | tf_op jit(solution)/shard_map/all_to_all | solution.py:53
  86.9 31.7 %all-to-all-start = ((bf16[4,1024,256]{2,0,1:T(4,128)(2,1)}), bf16[4,1024,256]{2,0,1:T(4,128)(2,1)}, u32[]{:S(2)}, u32[]{:S(2)}) async-start(bf16[4,1024,256]{2,0,1:T(4,128)(2,1)} %copy.17), calls=%async_computation | async-start | bytes 4194304 | tf_op jit(solution)/shard_map/all_to_all | solution.py:54
  91.3 201.5 %reduce-scatter.2.cloned.1.call-start = ((), (), s32[]{:S(2)}) async-start(), calls=%async_computation.5 | async-start | bytes 10485760 | tf_op jit(solution)/shard_map/reduce_scatter | solution.py:58
Sparse Core Ops, SparseCore 0:
  146.8 146.0 reduce-scatter.1
